TPU v7x, 32 devices: a whole 2x2x4 slice. The times are simulated.
32 devices in a mesh: dp: 16 (over z, y, x), mp: 2 (over core).
Axes of the slice: x: 2, y: 2, z: 4, core: 2. Of those that a mesh axis runs over, the one named last changes fastest.
Arguments:
- belief: bfloat16 [4096, 2652], P('dp'), may hold values from -6 to 6
- target_value: bfloat16 [4096, 1326], P('dp'), may hold values from -6 to 6
- counts: int32 [32], P('dp'), may hold values from 1 to 128, as said below
- w_first: bfloat16 [2652, 1536], P(None, 'mp'), may hold values from -0.125 to 0.125
- w_middle: bfloat16 [1536, 1536], P('mp'), may hold values from -0.15625 to 0.15625
- w_last: bfloat16 [1536, 1326], P(None, 'mp'), may hold values from -0.15625 to 0.15625
Outputs:
- grad_first: float32 [2652, 1536], P(None, ('mp', 'dp'))
- grad_middle: float32 [1536, 1536], P('mp', 'dp')
- grad_last: float32 [1536, 1326], P('dp', 'mp')
Inputs may be any that keep to these rules, and one draw needn't show every extreme that they name: `counts`: rows past a subgame's count in its block are padding with arbitrary values.
All inputs are finite; a program needn't handle non-finite values.
Results may differ from a plain program's by a relative error of at most 0.0089.
Values may be sent and summed in bfloat16 or wider, within the bound.
A program may use at most 192 MiB of HBM per device.

v0:
```python
import jax
import jax.numpy as jnp
from jax import lax
from jax.sharding import PartitionSpec as P

BLOCK = 128
PARAMS = 8469504


def silu_slope(pre_act):
    sigmoid_of = jax.nn.sigmoid(pre_act)
    return sigmoid_of * (1.0 + pre_act * (1.0 - sigmoid_of))


def rows_grads(belief, target_value, live_mask, w_first, w_middle, w_last):
    pre_first = jnp.dot(belief, w_first, preferred_element_type=jnp.float32)
    act_first = jax.nn.silu(pre_first).astype(jnp.bfloat16)
    partial_middle = jnp.dot(act_first, w_middle, preferred_element_type=jnp.float32)
    pre_middle = lax.psum(partial_middle, "mp")
    act_middle = jax.nn.silu(pre_middle).astype(jnp.bfloat16)
    predicted = jnp.dot(act_middle, w_last, preferred_element_type=jnp.float32)
    mismatch = predicted - target_value.astype(jnp.float32)
    slope_out = (jnp.clip(mismatch, -1.0, 1.0) * live_mask[:, None]).astype(jnp.bfloat16)
    raw_last = jnp.dot(act_middle.T, slope_out, preferred_element_type=jnp.float32)
    partial_back = jnp.dot(slope_out, w_last.T, preferred_element_type=jnp.float32)
    back_middle = lax.psum(partial_back, "mp")
    slope_middle = (back_middle * silu_slope(pre_middle)).astype(jnp.bfloat16)
    raw_middle = jnp.dot(act_first.T, slope_middle, preferred_element_type=jnp.float32)
    back_first = jnp.dot(slope_middle, w_middle.T, preferred_element_type=jnp.float32)
    slope_first = (back_first * silu_slope(pre_first)).astype(jnp.bfloat16)
    raw_first = jnp.dot(belief.T, slope_first, preferred_element_type=jnp.float32)
    return (raw_first, raw_middle, raw_last)


def per_device(belief, target_value, counts, w_first, w_middle, w_last):
    total_rows = belief.shape[0]
    own_width = w_last.shape[1]
    target_value = lax.dynamic_slice_in_dim(
        target_value, lax.axis_index("mp") * own_width, own_width, 1
    )
    live_rows = (counts[:, None] > jnp.arange(BLOCK, dtype=jnp.int32)[None, :]).reshape(total_rows)
    raw_first, raw_middle, raw_last = rows_grads(
        belief, target_value, live_rows.astype(jnp.float32), w_first, w_middle, w_last
    )
    shard_first, shard_middle = (
        lax.psum_scatter(raw_first, "dp", scatter_dimension=1, tiled=True),
        lax.psum_scatter(raw_middle, "dp", scatter_dimension=1, tiled=True),
    )
    shard_last = lax.psum_scatter(raw_last, "dp", scatter_dimension=0, tiled=True)
    local_squares = (
        jnp.sum(shard_first * shard_first)
        + jnp.sum(shard_middle * shard_middle)
        + jnp.sum(shard_last * shard_last)
    )
    square_sum = lax.psum(local_squares, ("dp", "mp"))
    norm_scale = lax.rsqrt(square_sum / PARAMS + 1e-06)
    return (shard_first * norm_scale, shard_middle * norm_scale, shard_last * norm_scale)


def solution(mesh):
    return jax.shard_map(
        per_device,
        mesh=mesh,
        in_specs=(
            P("dp", None),
            P("dp", None),
            P("dp"),
            P(None, "mp"),
            P("mp", None),
            P(None, "mp"),
        ),
        out_specs=(P(None, ("mp", "dp")), P("mp", "dp"), P("dp", "mp")),
        check_vma=False,
    )
```

profile of v0, /device:TPU:0, one launch (start us, length us, event | category | flops | bytes accessed | tf_op | source)
XLA Modules:
  0.0 581.0 jit_solution(4656108067650917837)
XLA Ops:
  7.2 4.0 fusion.14
  11.3 0.9 copy-done.1
  12.2 2.0 fusion.12
  14.9 22.5 %all-reduce.3.cloned.1.call-done = f32[256,1536]{1,0:T(8,128)} async-done(((f32[256,1536]{1,0:T(8,128)}), f32[256,1536]{1,0:T(8,128)}) %all-reduce.3.cloned.1.call-update) | async-done | bytes 1572880 | tf_op jit(solution)/shard_map/psum | solution.py:19
  37.4 3.0 fusion.3
  40.4 1.9 fusion.15
  42.5 4.7 fusion.13
  47.2 16.9 %all-reduce.5.cloned.1.call-done = f32[256,1536]{1,0:T(8,128)} async-done(((f32[256,1536]{1,0:T(8,128)}), f32[256,1536]{1,0:T(8,128)}) %all-reduce.5.cloned.1.call-update) | async-done | bytes 1572880 | tf_op jit(solution)/shard_map/psum | solution.py:26
  64.1 2.4 multiply_convert_fusion
  66.6 4.2 fusion.11
  70.8 6.8 %convolution_bitcast_fusion = f32[2652,768]{1,0:T(8,128)} fusion(bf16[256,2652]{0,1:T(8,128)(2,1)} %param.6, bf16[256,1536]{1,0:T(8,128)(2,1)S(1)} %multiply_convert_fusion, bf16[768,1536]{1,0:T(8,128)(2,1)S(1)} %copy-done, f32[256,768]{1,0:T(8,128)} %copy-done.1), kind=kOutput, calls=%fused_computation | convolution fusion | flops 1648558080 | bytes 13436928 | tf_op jit(solution)/shard_map/dot_general | solution.py:31
  77.6 8.9 %copy.11 = f32[2652,768]{0,1:T(8,128)} copy(f32[2652,768]{1,0:T(8,128)} %convolution_bitcast_fusion) | data formatting | bytes 16293888
  86.6 123.3 %reduce-scatter.8.cloned.1.call-done = f32[96,663]{1,0:T(8,128)} async-done(((f32[1536,663]{1,0:T(8,128)}), f32[96,663]{1,0:T(8,128)}) %reduce-scatter.8.cloned.1.call-update) | async-done | bytes 254608 | tf_op jit(solution)/shard_map/reduce_scatter | solution.py:49
  209.8 1.6 multiply_reduce_fusion.1
  211.5 141.6 %reduce-scatter.6.cloned.1.call-done = f32[768,96]{0,1:T(8,128)} async-done(((f32[768,1536]{0,1:T(8,128)}), f32[768,96]{0,1:T(8,128)}) %reduce-scatter.6.cloned.1.call-update) | async-done | bytes 294928 | tf_op jit(solution)/shard_map/reduce_scatter | solution.py:47
  353.1 1.6 multiply_reduce_fusion.2
  354.7 166.2 %reduce-scatter.10.cloned.1.call-done = f32[48,2652]{1,0:T(8,128)} async-done(((f32[768,2652]{1,0:T(8,128)}), f32[48,2652]{1,0:T(8,128)}) %reduce-scatter.10.cloned.1.call-update) | async-done | bytes 509200
  521.0 2.5 copy.12
  523.5 2.3 multiply_reduce_fusion
  527.7 39.5 %psum.23 = f32[]{:T(128)} all-reduce(f32[]{:T(128)S(6)} %add.46), channel_id=1, replica_groups=mesh['dp'=16,'mp'=2] {'dp','mp'}, use_global_device_ids=true, to_apply=%region_8.9 | all-reduce | flops 1 | bytes 8 | tf_op jit(solution)/shard_map/psum | solution.py:55
  567.9 2.5 broadcast_multiply_fusion
  570.4 2.6 copy.10
  573.0 0.7 broadcast_multiply_fusion.1
  573.8 0.7 broadcast_multiply_fusion.2
  (24 shorter events, 1.0 us)
Async XLA Ops:
  7.2 5.0 copy-start
  7.2 30.2 %all-reduce.3.cloned.1.call-start = ((), (), s32[]{:S(2)}) async-start(), calls=%async_computation.3 | async-start | bytes 3145728 | tf_op jit(solution)/shard_map/psum | solution.py:19
  11.3 0.9 copy-start.1
  14.1 0.7 copy-start.6
  14.1 23.3 %copy-start.5 = (bf16[256,1326]{0,1:T(8,128)(2,1)S(1)}, bf16[256,1326]{0,1:T(8,128)(2,1)}, u32[]{:S(2)}) copy-start(bf16[256,1326]{0,1:T(8,128)(2,1)} %param.7) | copy-start | bytes 2036740
  14.2 50.0 %all-reduce.5.cloned.1.call-start = ((), (), s32[]{:S(2)}) async-start(), calls=%async_computation.4 | async-start | bytes 3145728 | tf_op jit(solution)/shard_map/psum | solution.py:26
  37.4 3.0 copy-start.2
  42.4 167.4 %reduce-scatter.8.cloned.1.call-start = ((), (), s32[]{:S(2)}) async-start(), calls=%async_computation.6 | async-start | bytes 5013504 | tf_op jit(solution)/shard_map/reduce_scatter | solution.py:49
  47.1 305.9 %reduce-scatter.6.cloned.1.call-start = ((), (), s32[]{:S(2)}) async-start(), calls=%async_computation.5 | async-start | bytes 5013504 | tf_op jit(solution)/shard_map/reduce_scatter | solution.py:47
  70.8 450.2 %reduce-scatter.10.cloned.1.call-start = ((), (), s32[]{:S(2)}) async-start(), calls=%async_computation.7 | async-start | bytes 8773632
  570.4 2.6 copy-start.3
  570.4 3.3 copy-start.4
Sparse Core Ops, SparseCore 0:
  14.3 23.0 all-reduce.2
  42.5 21.5 all-reduce.4
  69.3 140.4 reduce-scatter.7
  214.9 138.1 reduce-scatter.5
  358.5 162.3 reduce-scatter.9
where the time goes:
time: 582 us; the launch traced here: 581 us
  waiting for transfers between devices  471 us (81%)
  blocking collectives  39.5 us (7%)
  matrix products  26.6 us (5%)
  between operations  16.5 us (3%)
  local copies, waits for them, and re-layouts  15.6 us (3%)
  other arithmetic  12 us (2%)
    unnamed x6, waiting for transfers between devices  166 us
    reduce_scatter x1, waiting for transfers between devices, per_device(): lax.psum_scatter(raw_middle, 'dp', scatter_dimension=1, tiled=True)  142 us
    reduce_scatter x1, waiting for transfers between devices, per_device(): lax.psum_scatter(raw_last, 'dp', scatter_dimension=0, tiled=True)  123 us
    psum x1, blocking collectives, per_device(): square_sum = lax.psum(local_squares, ('dp', 'mp'))  39.5 us
    psum x1, waiting for transfers between devices, rows_grads(): pre_middle = lax.psum(partial_middle, 'mp')  22.5 us
    psum x1, waiting for transfers between devices, rows_grads(): back_middle = lax.psum(partial_back, 'mp')  16.9 us
    unnamed x17, local copies, waits for them, and re-layouts  15.6 us
  transfers between devices with their start and end apart: 5, of which 5 were waited for; matrix products, arithmetic and copies ran while one was open for 5% of the time, Pallas kernels for 0%

commit v1 on v0

v1 whole, which is shorter than its diff:
```python
import functools

import jax
import jax.numpy as jnp
from jax import lax
from jax.experimental import pallas as pl
from jax.experimental.pallas import tpu as pltpu
from jax.sharding import PartitionSpec as P

BLOCK = 128
LANES = 128
MESH = pl.DeviceIdType.MESH


def silu_slope(pre_act):
    sigmoid_of = jax.nn.sigmoid(pre_act)
    return sigmoid_of * (1.0 + pre_act * (1.0 - sigmoid_of))


def pad_to(size, step):
    return -(-size // step) * step


def cut_pieces(shapes, cuts):
    pairs = []
    for which, parts in cuts:
        tiles = shapes[which][-1] // LANES
        bounds = [round(tiles * i / (2 * parts)) * LANES for i in range(2 * parts + 1)]
        for i in range(parts):
            pairs.append(
                tuple(
                    (which, bounds[2 * i + t], bounds[2 * i + t + 1] - bounds[2 * i + t])
                    for t in range(2)
                )
            )
    return pairs


def scatter_kernel(dims, params, pairs, *refs):
    n_dp, n_mp = dims
    far = n_dp // 4
    count = len(pairs)
    flat = 2 * count
    grads, outs = refs[:3], refs[3:6]
    got1, sum1, got2, sum2, got3 = (refs[6 + k * flat : 6 + (k + 1) * flat] for k in range(5))
    sq_send, sq_got, send_sems, got_sems, far_send, far_got, sq_sems = refs[6 + 5 * flat :]

    dp, mp = lax.axis_index("dp"), lax.axis_index("mp")
    low, mid, top = dp % 2, (dp // 2) % 2, dp // 4
    me = dp * n_mp + mp
    total = n_dp * n_mp

    barrier = pltpu.get_barrier_semaphore()

    def greet(j, _):
        other = lax.rem(me + j, total)
        pl.semaphore_signal(
            barrier, inc=1, device_id=(other // n_mp, other % n_mp), device_id_type=MESH
        )
        return 0

    lax.fori_loop(1, total, greet, 0)
    pl.semaphore_wait(barrier, total - 1)

    low_peer = (dp + 1 - 2 * low, mp)
    mid_peer = (dp + 2 - 4 * mid, mp)

    def copy1(p, t):
        which, start, width = pairs[p][t]
        cols = pl.ds(start, width)
        src = (
            grads[which].at[:, :, 1 - low, :, cols]
            if t == 0
            else grads[which].at[:, 1 - mid, :, :, cols]
        )
        k = 2 * p + t
        return pltpu.make_async_remote_copy(
            src, got1[k], send_sems.at[0, k], got_sems.at[0, k],
            device_id=low_peer if t == 0 else mid_peer, device_id_type=MESH,
        )

    def copy2(p, t):
        k = 2 * p + t
        return pltpu.make_async_remote_copy(
            sum1[k].at[:, (1 - mid) if t == 0 else (1 - low)], got2[k],
            send_sems.at[1, k], got_sems.at[1, k],
            device_id=mid_peer if t == 0 else low_peer, device_id_type=MESH,
        )

    def copy3(p, t, j):
        k = 2 * p + t
        goal = lax.rem(top + j, far)
        return pltpu.make_async_remote_copy(
            sum2[k].at[goal], got3[k].at[j - 1], far_send.at[k, j - 1], far_got.at[k, j - 1],
            device_id=(dp + (goal - top) * 4, mp), device_id_type=MESH,
        )

    def add1(p, t):
        which, start, width = pairs[p][t]
        k = 2 * p + t

        def body(i, _):
            z, b = i // 2, i % 2
            own = (
                grads[which][z, b, low, :, start : start + width]
                if t == 0
                else grads[which][z, mid, b, :, start : start + width]
            )
            both = own.astype(jnp.float32) + got1[k][z, b].astype(jnp.float32)
            sum1[k][z, b] = both.astype(jnp.bfloat16)
            return 0

        lax.fori_loop(0, 2 * far, body, 0)

    def add2(p, t):
        k = 2 * p + t
        side = mid if t == 0 else low

        def body(z, _):
            both = sum1[k][z, side].astype(jnp.float32) + got2[k][z].astype(jnp.float32)
            sum2[k][z] = both.astype(jnp.bfloat16)
            return 0

        lax.fori_loop(0, far, body, 0)

    for p in range(min(2, count)):
        for t in range(2):
            copy1(p, t).start()
    for i in range(count + 1):
        if i < count:
            for t in range(2):
                copy1(i, t).wait_recv()
                add1(i, t)
                copy2(i, t).start()
            if i + 2 < count:
                for t in range(2):
                    copy1(i + 2, t).start()
        if i >= 1:
            for t in range(2):
                copy2(i - 1, t).wait_recv()
                add2(i - 1, t)
                for j in range(1, far):
                    copy3(i - 1, t, j).start()
    squares = jnp.float32(0.0)
    for p in range(count):
        for t in range(2):
            which, start, width = pairs[p][t]
            k = 2 * p + t
            value = sum2[k][top].astype(jnp.float32)
            for j in range(1, far):
                copy3(p, t, j).wait_recv()
                value = value + got3[k][j - 1].astype(jnp.float32)
            outs[which][:, start : start + width] = value
            squares = squares + jnp.sum(value * value)

    sq_send[...] = jnp.full(sq_send.shape, squares, jnp.float32)

    def share_copy(j):
        other = lax.rem(me + j, total)
        return pltpu.make_async_remote_copy(
            sq_send, sq_got.at[j - 1], sq_sems.at[0], sq_sems.at[1],
            device_id=(other // n_mp, other % n_mp), device_id_type=MESH,
        )

    def share(j, _):
        share_copy(j).start()
        return 0

    lax.fori_loop(1, total, share, 0)
    pltpu.make_async_copy(sq_got, sq_got, sq_sems.at[1]).wait()
    everyone = squares + jnp.sum(sq_got[...]) * (1.0 / (sq_send.shape[0] * sq_send.shape[1]))
    scale = lax.rsqrt(jnp.full((1, LANES), everyone / params + 1e-06, jnp.float32))
    for p in range(count):
        for t in range(2):
            which, start, width = pairs[p][t]
            for c in range(start, start + width, LANES):
                outs[which][:, c : c + LANES] = outs[which][:, c : c + LANES] * scale

    for p in range(count):
        for t in range(2):
            copy1(p, t).wait_send()
            copy2(p, t).wait_send()
            for j in range(1, far):
                copy3(p, t, j).wait_send()
    pltpu.make_async_copy(sq_got, sq_got, sq_sems.at[0]).wait()


def scatter_grads(dims, params, grads, cuts):
    n_dp, n_mp = dims
    far = n_dp // 4
    grads = [
        jnp.pad(g.astype(jnp.bfloat16), ((0, 0), (0, pad_to(g.shape[1], LANES) - g.shape[1])))
        .reshape(far, 2, 2, g.shape[0] // n_dp, pad_to(g.shape[1], LANES))
        for g in grads
    ]
    shapes = [g.shape for g in grads]
    pairs = cut_pieces(shapes, cuts)

    def buffers(lead):
        return [
            pltpu.VMEM(lead + (shapes[piece[0]][3], piece[2]), jnp.bfloat16)
            for pair in pairs
            for piece in pair
        ]

    flat = 2 * len(pairs)
    spec = pl.BlockSpec(memory_space=pltpu.VMEM)
    return pl.pallas_call(
        functools.partial(scatter_kernel, dims, params, pairs),
        out_shape=[jax.ShapeDtypeStruct(s[3:], jnp.float32) for s in shapes],
        in_specs=[spec] * 3,
        out_specs=[spec] * 3,
        scratch_shapes=(
            buffers((far, 2)) + buffers((far, 2)) + buffers((far,)) + buffers((far,))
            + buffers((far - 1,))
            + [
                pltpu.VMEM((8, LANES), jnp.float32),
                pltpu.VMEM((n_dp * n_mp - 1, 8, LANES), jnp.float32),
                pltpu.SemaphoreType.DMA((2, flat)),
                pltpu.SemaphoreType.DMA((2, flat)),
                pltpu.SemaphoreType.DMA((flat, far - 1)),
                pltpu.SemaphoreType.DMA((flat, far - 1)),
                pltpu.SemaphoreType.DMA((2,)),
            ]
        ),
        compiler_params=pltpu.CompilerParams(
            collective_id=0, has_side_effects=True, vmem_limit_bytes=60 * 1024 * 1024
        ),
    )(*grads)


def per_device(dims, belief, target_value, counts, w_first, w_middle, w_last):
    n_dp, n_mp = dims
    total_rows = belief.shape[0]
    own_width = w_last.shape[1]
    params = float(n_mp * (w_first.size + w_middle.size + w_last.size))
    target_value = lax.dynamic_slice_in_dim(
        target_value, lax.axis_index("mp") * own_width, own_width, 1
    )
    live_rows = (counts[:, None] > jnp.arange(BLOCK, dtype=jnp.int32)[None, :]).reshape(total_rows)
    live_mask = live_rows.astype(jnp.float32)

    pre_first = jnp.dot(belief, w_first, preferred_element_type=jnp.float32)
    act_first = jax.nn.silu(pre_first).astype(jnp.bfloat16)
    partial_middle = jnp.dot(act_first, w_middle, preferred_element_type=jnp.float32)
    pre_middle = lax.psum(partial_middle, "mp")
    act_middle = jax.nn.silu(pre_middle).astype(jnp.bfloat16)
    predicted = jnp.dot(act_middle, w_last, preferred_element_type=jnp.float32)
    mismatch = predicted - target_value.astype(jnp.float32)
    slope_out = (jnp.clip(mismatch, -1.0, 1.0) * live_mask[:, None]).astype(jnp.bfloat16)
    raw_last = jnp.dot(act_middle.T, slope_out, preferred_element_type=jnp.float32)
    partial_back = jnp.dot(slope_out, w_last.T, preferred_element_type=jnp.float32)
    back_middle = lax.psum(partial_back, "mp")
    slope_middle = (back_middle * silu_slope(pre_middle)).astype(jnp.bfloat16)
    raw_middle = jnp.dot(slope_middle.T, act_first, preferred_element_type=jnp.float32)
    back_first = jnp.dot(slope_middle, w_middle.T, preferred_element_type=jnp.float32)
    slope_first = (back_first * silu_slope(pre_first)).astype(jnp.bfloat16)
    raw_first = jnp.dot(slope_first.T, belief, preferred_element_type=jnp.float32)

    first, middle, last = scatter_grads(
        dims, params, (raw_first, raw_middle, raw_last), ((2, 1), (1, 1), (0, 2))
    )
    return first[:, : belief.shape[1]].T, middle.T, last[:, :own_width]


def solution(mesh):
    return jax.shard_map(
        functools.partial(per_device, (mesh.shape["dp"], mesh.shape["mp"])),
        mesh=mesh,
        in_specs=(
            P("dp", None),
            P("dp", None),
            P("dp"),
            P(None, "mp"),
            P("mp", None),
            P(None, "mp"),
        ),
        out_specs=(P(None, ("mp", "dp")), P("mp", "dp"), P("dp", "mp")),
        check_vma=False,
    )
```

time: 582 us -> 203 us (0.35)
  waiting for transfers between devices: 471 us -> 33.2 us
  Pallas kernels: 0 us -> 105 us
  blocking collectives: 39.5 us -> 0 us
  other arithmetic: 12 us -> 2.51 us
  local copies, waits for them, and re-layouts: 15.6 us -> 24.1 us
    reduce_scatter x2 -> x0, waiting for transfers between devices: 265 us -> none  [the longest x1 142 us: per_device(): lax.psum_scatter(raw_middle, 'dp', scatter_dimension=1, tiled=True)]
    unnamed x6 -> x2, waiting for transfers between devices: 166 us -> 0.03 us
    pallas_call x0 -> x1, Pallas kernels: none -> 105 us  [scatter_grads(): pl.pallas_call(functools.partial(scatter_kernel, dims, params, pairs), ou...]
    psum x1 -> x0, blocking collectives: 39.5 us -> none  [per_device(): square_sum = lax.psum(local_squares, ('dp', 'mp'))]
    pad x0 -> x2, local copies, waits for them, and re-layouts: none -> 7.77 us  [scatter_grads(): jnp.pad(g.astype(jnp.bfloat16), ((0, 0), (0, pad_to(g.shape[1], LANES) -...]
    psum x2, waiting for transfers between devices: 39.5 us -> 33.2 us  [the longest x1 22.5 us: per_device(): pre_middle = lax.psum(partial_middle, 'mp')]
    unnamed x17 -> x16, local copies, waits for them, and re-layouts: 15.6 us -> 14.4 us
  transfers between devices with their start and end apart: 5 -> 2, of which waited for: 5 -> 2; matrix products, arithmetic and copies ran while one was open for 5% -> 5% of each run, Pallas kernels for 0% -> 0%
where the time goes in v1:
time: 203 us
  Pallas kernels  105 us (52%)
  waiting for transfers between devices  33.2 us (16%)
  local copies, waits for them, and re-layouts  24.1 us (12%)
  matrix products  23.4 us (12%)
  between operations  14.1 us (7%)
  other arithmetic  2.51 us (1%)
    pallas_call x1, Pallas kernels, scatter_grads(): pl.pallas_call(functools.partial(scatter_kernel, dims, params, pairs), ou...  105 us
    psum x1, waiting for transfers between devices, per_device(): pre_middle = lax.psum(partial_middle, 'mp')  22.5 us
    unnamed x16, local copies, waits for them, and re-layouts  14.4 us
    psum x1, waiting for transfers between devices, per_device(): back_middle = lax.psum(partial_back, 'mp')  10.7 us
    pad x2, local copies, waits for them, and re-layouts, scatter_grads(): jnp.pad(g.astype(jnp.bfloat16), ((0, 0), (0, pad_to(g.shape[1], LANES) -...  7.77 us
    dot_general x1, matrix products, per_device(): jnp.dot(slope_first.T, belief, preferred_element_type=jnp.float32)  5.51 us
  transfers between devices with their start and end apart: 2, of which 2 were waited for; matrix products, arithmetic and copies ran while one was open for 5% of the time, Pallas kernels for 0%

profile of v1, /device:TPU:0, one launch (start us, length us, event | category | flops | bytes accessed | tf_op | source)
XLA Modules:
  0.0 202.7 jit_solution(17366347362816868350)
XLA Ops:
  7.2 0.0 all-reduce.5.cloned.1.call-start
  7.2 4.0 %fusion.12 = f32[256,768]{1,0:T(8,128)S(1)} fusion(bf16[256,2652]{0,1:T(8,128)(2,1)} %param.6, bf16[2652,768]{1,0:T(8,128)(2,1)} %param.9), kind=kOutput, calls=%fused_computation.24 | convolution fusion | flops 1042808832 | bytes 6217728 | tf_op jit(solution)/shard_map/dot_general | solution.py:243
  11.3 0.9 copy-done.5
  12.2 2.0 fusion.11
  14.2 0.0 all-reduce.5.cloned.1.call-update
  14.2 0.0 all-reduce.7.cloned.1.call-start
  14.3 0.6 copy-done.4
  14.8 0.1 fusion.9
  14.9 22.5 %all-reduce.5.cloned.1.call-done = f32[256,1536]{1,0:T(8,128)} async-done(((f32[256,1536]{1,0:T(8,128)}), f32[256,1536]{1,0:T(8,128)}) %all-reduce.5.cloned.1.call-update) | async-done | bytes 1572880 | tf_op jit(solution)/shard_map/psum | solution.py:246
  37.5 3.0 %fusion.3 = bf16[256,663]{0,1:T(8,128)(2,1)S(1)} fusion(bf16[1536,663]{0,1:T(8,128)(2,1)} %param.11, f32[256]{0:T(256)S(1)} %fusion.9, bf16[256,1326]{0,1:T(8,128)(2,1)S(1)} %copy-done.3, s32[]{:T(128)S(6)} %select_n.3, f32[256,1536]{1,0:T(8,128)} %all-reduce.5.cloned.1.call-done), kind=kOutput, calls=%fused_computation.11 | convolution fusion | flops 524219136 | bytes 4289540 | tf_op jit(solution)/shard_map/dot_general | solution.py:248
  40.5 2.0 fusion.13
  42.5 3.5 %convolution_convert_fusion.2 = bf16[1536,663]{0,1:T(8,128)(2,1)} fusion(bf16[256,663]{0,1:T(8,128)(2,1)S(1)} %fusion.3, f32[256,1536]{1,0:T(8,128)} %all-reduce.5.cloned.1.call-done), kind=kOutput, calls=%fused_computation.2 | convolution fusion | flops 524388864 | bytes 3949056 | tf_op jit(solution)/shard_map/dot_general | solution.py:251
  46.0 4.1 %copy.12 = bf16[1536,663]{1,0:T(8,128)(2,1)} copy(bf16[1536,663]{0,1:T(8,128)(2,1)} %convolution_convert_fusion.2) | data formatting | bytes 4073472
  50.1 3.4 %pad.9.clone = bf16[1536,768]{1,0:T(8,128)(2,1)} pad(bf16[1536,663]{1,0:T(8,128)(2,1)} %copy.12, bf16[]{:T(256)} %constant.6.clone.1), padding=0_0x0_105 | pad | bytes 4396034 | tf_op jit(solution)/shard_map/jit(_pad)/pad | solution.py:192
  53.5 10.7 %all-reduce.7.cloned.1.call-done = f32[256,1536]{1,0:T(8,128)} async-done(((f32[256,1536]{1,0:T(8,128)}), f32[256,1536]{1,0:T(8,128)}) %all-reduce.7.cloned.1.call-update) | async-done | bytes 1572880 | tf_op jit(solution)/shard_map/psum | solution.py:253
  64.2 2.4 %multiply_convert_fusion = bf16[256,1536]{1,0:T(8,128)(2,1)S(1)} fusion(f32[256,1536]{1,0:T(8,128)} %all-reduce.7.cloned.1.call-done, f32[256,1536]{1,0:T(8,128)} %all-reduce.5.cloned.1.call-done), kind=kLoop, calls=%fused_computation.3 | loop fusion | flops 3538944 | bytes 3932160 | tf_op jit(solution)/shard_map/convert_element_type | solution.py:254
  66.6 5.5 %convolution_convert_fusion = bf16[768,2652]{0,1:T(8,128)(2,1)} fusion(bf16[256,2652]{0,1:T(8,128)(2,1)} %param.6, bf16[256,1536]{1,0:T(8,128)(2,1)S(1)} %multiply_convert_fusion, bf16[768,1536]{1,0:T(8,128)(2,1)S(1)} %copy-done, f32[256,768]{1,0:T(8,128)} %copy-done.5), kind=kOutput, calls=%fused_computation | convolution fusion | flops 1650594816 | bytes 9363456 | tf_op jit(solution)/shard_map/dot_general | solution.py:258
  72.1 3.4 %convolution_convert_fusion.1 = bf16[1536,768]{1,0:T(8,128)(2,1)} fusion(bf16[256,1536]{1,0:T(8,128)(2,1)S(1)} %multiply_convert_fusion, f32[256,768]{1,0:T(8,128)} %copy-done.5), kind=kOutput, calls=%fused_computation.1 | convolution fusion | flops 606142464 | bytes 3932160 | tf_op jit(solution)/shard_map/dot_general | solution.py:255
  75.5 6.4 %copy.11 = bf16[768,2652]{1,0:T(8,128)(2,1)} copy(bf16[768,2652]{0,1:T(8,128)(2,1)} %convolution_convert_fusion) | data formatting | bytes 8146944
  81.9 4.4 %pad.8.clone = bf16[768,2688]{1,0:T(8,128)(2,1)} pad(bf16[768,2652]{1,0:T(8,128)(2,1)} %copy.11, bf16[]{:T(256)} %constant.6.clone.1), padding=0_0x0_36 | pad | bytes 8202242 | tf_op jit(solution)/shard_map/jit(_pad)/pad | solution.py:192
  86.3 105.3 %shard_map.85 = (f32[48,2688]{1,0:T(8,128)}, f32[96,768]{1,0:T(8,128)}, f32[96,768]{1,0:T(8,128)}) custom-call(bf16[4,2,2,48,2688]{4,3,2,1,0:T(8,128)(2,1)} %bitcast.20, bf16[4,2,2,96,768]{4,3,2,1,0:T(8,128)(2,1)} %bitcast.22, bf16[4,2,2,96,768]{4,3,2,1,0:T(8,128)(2,1)} %bitcast.21), custom_call_target="tpu_custom_call" | custom-call | tf_op jit(solution)/shard_map/pallas_call | solution.py:208
  191.6 1.9 slice_bitcast_fusion
  193.5 1.7 copy.17
  195.2 0.7 copy.18
  (11 shorter events, 0.0 us)
Async XLA Ops:
  7.2 5.0 %copy-start = (bf16[768,1536]{1,0:T(8,128)(2,1)S(1)}, bf16[768,1536]{1,0:T(8,128)(2,1)}, u32[]{:S(2)}) copy-start(bf16[768,1536]{1,0:T(8,128)(2,1)} %param.10) | copy-start | bytes 7077892
  7.2 30.3 %all-reduce.5.cloned.1.call-start = ((), (), s32[]{:S(2)}) async-start(), calls=%async_computation | async-start | bytes 3145728 | tf_op jit(solution)/shard_map/psum | solution.py:246
  11.3 0.9 copy-start.5
  14.2 0.7 copy-start.4
  14.2 23.3 %copy-start.3 = (bf16[256,1326]{0,1:T(8,128)(2,1)S(1)}, bf16[256,1326]{0,1:T(8,128)(2,1)}, u32[]{:S(2)}) copy-start(bf16[256,1326]{0,1:T(8,128)(2,1)} %param.7) | copy-start | bytes 2036740
  14.2 50.0 %all-reduce.7.cloned.1.call-start = ((), (), s32[]{:S(2)}) async-start(), calls=%async_computation.1 | async-start | bytes 3145728 | tf_op jit(solution)/shard_map/psum | solution.py:253
  37.5 3.0 %copy-start.1 = (bf16[1536,663]{0,1:T(8,128)(2,1)S(1)}, bf16[1536,663]{0,1:T(8,128)(2,1)}, u32[]{:S(2)}) copy-start(bf16[1536,663]{0,1:T(8,128)(2,1)} %param.11) | copy-start | bytes 6110212
  191.5 3.6 %copy-start.2 = (f32[96,768]{1,0:T(8,128)S(1)}, f32[96,768]{1,0:T(8,128)}, u32[]{:S(2)}) copy-start(f32[96,768]{1,0:T(8,128)} %get-tuple-element.8) | copy-start | bytes 884740
Sparse Core Ops, SparseCore 0:
  14.3 23.0 all-reduce.4
  42.6 21.5 all-reduce.6

commit v2 on v1

--- a/solution.py
+++ b/solution.py
@@ -36,14 +36,28 @@
     return pairs
 
 
-def scatter_kernel(dims, params, pairs, *refs):
+def step_kernel(dims, params, pairs, blocks, *refs):
     n_dp, n_mp = dims
     far = n_dp // 4
     count = len(pairs)
     flat = 2 * count
-    grads, outs = refs[:3], refs[3:6]
-    got1, sum1, got2, sum2, got3 = (refs[6 + k * flat : 6 + (k + 1) * flat] for k in range(5))
-    sq_send, sq_got, send_sems, got_sems, far_send, far_got, sq_sems = refs[6 + 5 * flat :]
+    counts, loads, outs = refs[0], refs[1:6], refs[6:9]
+    refs = refs[9:]
+    got1, sum1, got2, sum2, got3 = (refs[k * flat : (k + 1) * flat] for k in range(5))
+    refs = refs[5 * flat :]
+    held, grads = refs[:5], refs[5:8]
+    (
+        pre1, act1, slope1_t, part2, other2, pre2, act2, act2_t, slope_last, part_back, other_back,
+        slope2, slope2_t, load_sems, swap_send, swap_got,
+        sq_send, sq_got, send_sems, got_sems, far_send, far_got, sq_sems,
+    ) = refs[8:]
+    belief, target, w_first, w_middle, w_last = held
+    arrivals = [
+        pltpu.make_async_copy(src, dst, load_sems.at[i])
+        for i, (src, dst) in enumerate(zip(loads, held))
+    ]
+    for i in (0, 2, 3, 4, 1):
+        arrivals[i].start()
 
     dp, mp = lax.axis_index("dp"), lax.axis_index("mp")
     low, mid, top = dp % 2, (dp // 2) % 2, dp // 4
@@ -123,18 +137,126 @@
 
         lax.fori_loop(0, far, body, 0)
 
-    for p in range(min(2, count)):
+    rows, hid = act2.shape
+    own_width = w_last.shape[1]
+    in_width = belief.shape[1]
+    block = hid // blocks
+
+    def swap(side, part, other, i):
+        return pltpu.make_async_remote_copy(
+            part.at[i], other.at[i], swap_send.at[side, i], swap_got.at[side, i],
+            device_id=(dp, 1 - mp), device_id_type=MESH,
+        )
+
+    def weight_grad(which, left_t, right, stop, start, width):
+        r = grads[which].shape[3]
+        real = min(width, stop - start)
+
+        def body(z, _):
+            at = pl.multiple_of(z * 4 * r, 16)
+            value = jnp.dot(
+                left_t[pl.ds(at, 4 * r), :], right[:, start : start + real],
+                preferred_element_type=jnp.float32,
+            )
+            if real < width:
+                value = jnp.concatenate(
+                    [value, jnp.zeros((4 * r, width - real), jnp.float32)], axis=1
+                )
+            for b in range(4):
+                grads[which][z, b // 2, b % 2, :, start : start + width] = value[
+                    b * r : (b + 1) * r
+                ].astype(jnp.bfloat16)
+            return 0
+
+        lax.fori_loop(0, far, body, 0)
+
+    def pair_grads(p, left_t, right, stop):
         for t in range(2):
+            which, start, width = pairs[p][t]
+            weight_grad(which, left_t, right, stop, start, width)
             copy1(p, t).start()
+
+    own_hid = act1.shape[1]
+    arrivals[0].wait()
+    arrivals[2].wait()
+    for c in range(0, own_hid, 256):
+        value = jnp.dot(
+            belief[...], w_first[:, c : c + 256], preferred_element_type=jnp.float32
+        )
+        pre1[:, c : c + 256] = value
+        act1[:, c : c + 256] = jax.nn.silu(value).astype(jnp.bfloat16)
+    arrivals[3].wait()
+    for i in range(blocks):
+        part2[i] = jnp.dot(
+            act1[...], w_middle[:, i * block : (i + 1) * block],
+            preferred_element_type=jnp.float32,
+        )
+        swap(0, part2, other2, i).start()
+    arrivals[1].wait()
+    arrivals[4].wait()
+    row = lax.broadcasted_iota(jnp.int32, (rows, 1), 0)
+    limit = jnp.full((rows, 1), counts[0], jnp.int32)
+    for b in range(1, rows // BLOCK):
+        limit = jnp.where(row >= b * BLOCK, counts[b] + b * BLOCK, limit)
+    live = jnp.where(row < limit, 1.0, 0.0)
+    for i in range(blocks):
+        cols = slice(i * block, (i + 1) * block)
+        swap(0, part2, other2, i).wait_recv()
+        value = part2[i] + other2[i]
+        pre2[:, cols] = value
+        act = jax.nn.silu(value)
+        act2[:, cols] = act.astype(jnp.bfloat16)
+        act2_t[cols, :] = act.astype(jnp.bfloat16).T
+    wanted = target[:, :own_width].astype(jnp.float32)
+    for m in range(1, n_mp):
+        wanted = jnp.where(
+            mp == m, target[:, m * own_width : (m + 1) * own_width].astype(jnp.float32), wanted
+        )
+    predicted = jnp.dot(act2[...], w_last[...], preferred_element_type=jnp.float32)
+    slope_last[...] = (jnp.clip(predicted - wanted, -1.0, 1.0) * live).astype(jnp.bfloat16)
+    for i in range(blocks):
+        part_back[i] = lax.dot_general(
+            slope_last[...], w_last[i * block : (i + 1) * block, :], (((1,), (1,)), ((), ())),
+            preferred_element_type=jnp.float32,
+        )
+        swap(1, part_back, other_back, i).start()
+    for p in range(count):
+        if pairs[p][0][0] == 2:
+            pair_grads(p, act2_t, slope_last, own_width)
+    for i in range(blocks):
+        cols = slice(i * block, (i + 1) * block)
+        swap(1, part_back, other_back, i).wait_recv()
+        value = (part_back[i] + other_back[i]) * silu_slope(pre2[:, cols])
+        slope2[:, cols] = value.astype(jnp.bfloat16)
+        slope2_t[cols, :] = value.astype(jnp.bfloat16).T
+    for p in range(count):
+        if pairs[p][0][0] == 1:
+            pair_grads(p, slope2_t, act1, own_hid)
+    for c in range(0, own_hid, 256):
+        back = lax.dot_general(
+            slope2[...], w_middle[c : c + 256, :], (((1,), (1,)), ((), ())),
+            preferred_element_type=jnp.float32,
+        )
+        value = back * silu_slope(pre1[:, c : c + 256])
+        slope1_t[c : c + 256, :] = value.astype(jnp.bfloat16).T
+    for i in range(blocks):
+        swap(0, part2, other2, i).wait_send()
+        swap(1, part_back, other_back, i).wait_send()
+
+    def first_grads(p):
+        if pairs[p][0][0] == 0:
+            pair_grads(p, slope1_t, belief, in_width)
+
+    for p in range(min(3, count)):
+        first_grads(p)
     for i in range(count + 1):
         if i < count:
             for t in range(2):
                 copy1(i, t).wait_recv()
                 add1(i, t)
                 copy2(i, t).start()
-            if i + 2 < count:
-                for t in range(2):
-                    copy1(i + 2, t).start()
+            if i + 3 < count:
+                first_grads(i + 3)
         if i >= 1:
             for t in range(2):
                 copy2(i - 1, t).wait_recv()
@@ -185,16 +307,18 @@
     pltpu.make_async_copy(sq_got, sq_got, sq_sems.at[0]).wait()
 
 
-def scatter_grads(dims, params, grads, cuts):
+def per_device(dims, belief, target_value, counts, w_first, w_middle, w_last):
     n_dp, n_mp = dims
     far = n_dp // 4
-    grads = [
-        jnp.pad(g.astype(jnp.bfloat16), ((0, 0), (0, pad_to(g.shape[1], LANES) - g.shape[1])))
-        .reshape(far, 2, 2, g.shape[0] // n_dp, pad_to(g.shape[1], LANES))
-        for g in grads
+    blocks = 3
+    rows, (in_width, own_hid) = belief.shape[0], w_first.shape
+    hid, own_width = w_last.shape
+    params = float(n_mp * (w_first.size + w_middle.size + w_last.size))
+    shapes = [
+        (far, 2, 2, long // n_dp, pad_to(wide, LANES))
+        for long, wide in ((own_hid, in_width), (hid, own_hid), (hid, own_width))
     ]
-    shapes = [g.shape for g in grads]
-    pairs = cut_pieces(shapes, cuts)
+    pairs = cut_pieces(shapes, ((2, 1), (1, 1), (0, 2)))
 
     def buffers(lead):
         return [
@@ -204,16 +328,37 @@
         ]
 
     flat = 2 * len(pairs)
-    spec = pl.BlockSpec(memory_space=pltpu.VMEM)
-    return pl.pallas_call(
-        functools.partial(scatter_kernel, dims, params, pairs),
+    loads = (belief, target_value, w_first, w_middle, w_last)
+    swapped = pltpu.VMEM((blocks, rows, hid // blocks), jnp.float32)
+    half, single = jnp.bfloat16, jnp.float32
+    first, middle, last = pl.pallas_call(
+        functools.partial(step_kernel, dims, params, pairs, blocks),
         out_shape=[jax.ShapeDtypeStruct(s[3:], jnp.float32) for s in shapes],
-        in_specs=[spec] * 3,
-        out_specs=[spec] * 3,
+        in_specs=[pl.BlockSpec(memory_space=pltpu.SMEM)]
+        + [pl.BlockSpec(memory_space=pl.ANY)] * 5,
+        out_specs=[pl.BlockSpec(memory_space=pltpu.VMEM)] * 3,
         scratch_shapes=(
             buffers((far, 2)) + buffers((far, 2)) + buffers((far,)) + buffers((far,))
             + buffers((far - 1,))
+            + [pltpu.VMEM(x.shape, x.dtype) for x in loads]
+            + [pltpu.VMEM(s, half) for s in shapes]
             + [
+                pltpu.VMEM((rows, own_hid), single),
+                pltpu.VMEM((rows, own_hid), half),
+                pltpu.VMEM((own_hid, rows), half),
+                swapped,
+                swapped,
+                pltpu.VMEM((rows, hid), single),
+                pltpu.VMEM((rows, hid), half),
+                pltpu.VMEM((hid, rows), half),
+                pltpu.VMEM((rows, own_width), half),
+                swapped,
+                swapped,
+                pltpu.VMEM((rows, hid), half),
+                pltpu.VMEM((hid, rows), half),
+                pltpu.SemaphoreType.DMA((5,)),
+                pltpu.SemaphoreType.DMA((2, blocks)),
+                pltpu.SemaphoreType.DMA((2, blocks)),
                 pltpu.VMEM((8, LANES), jnp.float32),
                 pltpu.VMEM((n_dp * n_mp - 1, 8, LANES), jnp.float32),
                 pltpu.SemaphoreType.DMA((2, flat)),
@@ -226,41 +371,8 @@
         compiler_params=pltpu.CompilerParams(
             collective_id=0, has_side_effects=True, vmem_limit_bytes=60 * 1024 * 1024
         ),
-    )(*grads)
-
-
-def per_device(dims, belief, target_value, counts, w_first, w_middle, w_last):
-    n_dp, n_mp = dims
-    total_rows = belief.shape[0]
-    own_width = w_last.shape[1]
-    params = float(n_mp * (w_first.size + w_middle.size + w_last.size))
-    target_value = lax.dynamic_slice_in_dim(
-        target_value, lax.axis_index("mp") * own_width, own_width, 1
-    )
-    live_rows = (counts[:, None] > jnp.arange(BLOCK, dtype=jnp.int32)[None, :]).reshape(total_rows)
-    live_mask = live_rows.astype(jnp.float32)
-
-    pre_first = jnp.dot(belief, w_first, preferred_element_type=jnp.float32)
-    act_first = jax.nn.silu(pre_first).astype(jnp.bfloat16)
-    partial_middle = jnp.dot(act_first, w_middle, preferred_element_type=jnp.float32)
-    pre_middle = lax.psum(partial_middle, "mp")
-    act_middle = jax.nn.silu(pre_middle).astype(jnp.bfloat16)
-    predicted = jnp.dot(act_middle, w_last, preferred_element_type=jnp.float32)
-    mismatch = predicted - target_value.astype(jnp.float32)
-    slope_out = (jnp.clip(mismatch, -1.0, 1.0) * live_mask[:, None]).astype(jnp.bfloat16)
-    raw_last = jnp.dot(act_middle.T, slope_out, preferred_element_type=jnp.float32)
-    partial_back = jnp.dot(slope_out, w_last.T, preferred_element_type=jnp.float32)
-    back_middle = lax.psum(partial_back, "mp")
-    slope_middle = (back_middle * silu_slope(pre_middle)).astype(jnp.bfloat16)
-    raw_middle = jnp.dot(slope_middle.T, act_first, preferred_element_type=jnp.float32)
-    back_first = jnp.dot(slope_middle, w_middle.T, preferred_element_type=jnp.float32)
-    slope_first = (back_first * silu_slope(pre_first)).astype(jnp.bfloat16)
-    raw_first = jnp.dot(slope_first.T, belief, preferred_element_type=jnp.float32)
-
-    first, middle, last = scatter_grads(
-        dims, params, (raw_first, raw_middle, raw_last), ((2, 1), (1, 1), (0, 2))
-    )
-    return first[:, : belief.shape[1]].T, middle.T, last[:, :own_width]
+    )(counts, *loads)
+    return first[:, :in_width].T, middle.T, last[:, :own_width]
 
 
 def solution(mesh):

time: 203 us -> 135 us (0.67)
  waiting for transfers between devices: 33.2 us -> 0 us
  matrix products: 23.4 us -> 0 us
  Pallas kernels: 105 us -> 122 us
  between operations: 14.1 us -> 0.65 us
  local copies, waits for them, and re-layouts: 24.1 us -> 12.6 us
  other arithmetic: 2.51 us -> 0 us
    psum x2 -> x0, waiting for transfers between devices: 33.2 us -> none  [the longest x1 22.5 us: per_device(): pre_middle = lax.psum(partial_middle, 'mp')]
    dot_general x7 -> x0, matrix products: 23.4 us -> none  [the longest x1 5.51 us: per_device(): jnp.dot(slope_first.T, belief, preferred_element_type=jnp.float32)]
    pallas_call x1, Pallas kernels: 105 us -> 122 us  [per_device(): pl.pallas_call(functools.partial(step_kernel, dims, params, pairs, blocks...]
    pad x2 -> x0, local copies, waits for them, and re-layouts: 7.77 us -> none  [scatter_grads(): jnp.pad(g.astype(jnp.bfloat16), ((0, 0), (0, pad_to(g.shape[1], LANES) -...]
    unnamed x16 -> x7, local copies, waits for them, and re-layouts: 14.4 us -> 10.7 us
    convert_element_type x2 -> x0, other arithmetic: 2.51 us -> none  [the longest x1 2.44 us: per_device(): slope_middle = (back_middle * silu_slope(pre_middle)).astype(jnp.bfloat16)]
  transfers between devices with their start and end apart: 2 -> 0, of which waited for: 2 -> 0; matrix products, arithmetic and copies ran while one was open for 5% -> 0% of each run, Pallas kernels for 0% -> 0%
where the time goes in v2:
time: 135 us
  Pallas kernels  122 us (90%)
  local copies, waits for them, and re-layouts  12.6 us (9%)
    pallas_call x1, Pallas kernels, per_device(): pl.pallas_call(functools.partial(step_kernel, dims, params, pairs, blocks...  122 us
    unnamed x7, local copies, waits for them, and re-layouts  10.7 us

profile of v2, /device:TPU:0, one launch (start us, length us, event | category | flops | bytes accessed | tf_op | source)
XLA Modules:
  0.0 134.7 jit_solution(4602420720103562224)
XLA Ops:
  0.6 0.0 copy-start
  0.6 2.4 %copy.10.refs_2_ = bf16[256,1326]{1,0:T(8,128)(2,1)} copy(bf16[256,1326]{0,1:T(8,128)(2,1)} %param.7) | data formatting | bytes 1357824 | tf_op args[1]
  3.0 2.5 %copy.9.refs_1_ = bf16[256,2652]{1,0:T(8,128)(2,1)} copy(bf16[256,2652]{0,1:T(8,128)(2,1)} %param.6) | data formatting | bytes 2715648 | tf_op args[0]
  5.5 0.0 copy-done
  5.5 2.4 %copy.11.refs_5_ = bf16[1536,663]{1,0:T(8,128)(2,1)} copy(bf16[1536,663]{0,1:T(8,128)(2,1)S(1)} %copy-done) | data formatting | bytes 4073472 | tf_op args[5]
  8.0 121.5 %shard_map.85 = (f32[48,2688]{1,0:T(8,128)}, f32[96,768]{1,0:T(8,128)}, f32[96,768]{1,0:T(8,128)}) custom-call(s32[2]{0:T(128)} %refs_0_.1, bf16[256,2652]{1,0:T(8,128)(2,1)} %copy.9.refs_1_, bf16[256,1326]{1,0:T(8,128)(2,1)} %copy.10.refs_2_, bf16[2652,768]{1,0:T(8,128)(2,1)} %refs_3_.1, bf16[768,1536]{1,0:T(8,128)(2,1)} %refs_4_.1, ...), custom_call_target="tpu_custom_call" | custom-call | tf_op jit(solution)/shard_map/pallas_call | solution.py:334
  129.5 1.9 %slice_bitcast_fusion = f32[2652,48]{0,1:T(8,128)} fusion(f32[48,2688]{1,0:T(8,128)} %get-tuple-element.6), kind=kLoop, calls=%fused_computation | loop fusion | bytes 1018368 | tf_op jit(solution)/shard_map/transpose | solution.py:375
  131.4 1.7 %copy.14 = f32[768,96]{0,1:T(8,128)} copy(f32[768,96]{0,1:T(8,128)} %bitcast.5) | data formatting | bytes 589824
  133.1 1.7 %copy.15 = f32[96,663]{1,0:T(8,128)} copy(f32[96,663]{1,0:T(8,128)} %bitcast.4) | data formatting | bytes 509184
Async XLA Ops:
  0.6 4.9 %copy-start = (bf16[1536,663]{0,1:T(8,128)(2,1)S(1)}, bf16[1536,663]{0,1:T(8,128)(2,1)}, u32[]{:S(2)}) copy-start(bf16[1536,663]{0,1:T(8,128)(2,1)} %param.11) | copy-start | bytes 6110212

commit v3 on v2

--- a/solution.py
+++ b/solution.py
@@ -318,7 +318,7 @@
         (far, 2, 2, long // n_dp, pad_to(wide, LANES))
         for long, wide in ((own_hid, in_width), (hid, own_hid), (hid, own_width))
     ]
-    pairs = cut_pieces(shapes, ((2, 1), (1, 1), (0, 2)))
+    pairs = cut_pieces(shapes, ((2, 1), (1, 1), (0, 4)))
 
     def buffers(lead):
         return [

time: 135 us -> 125 us (0.926)
  Pallas kernels: 122 us -> 111 us
    pallas_call x1, Pallas kernels: 122 us -> 111 us  [per_device(): pl.pallas_call(functools.partial(step_kernel, dims, params, pairs, blocks...]
where the time goes in v3:
time: 125 us
  Pallas kernels  111 us (89%)
  local copies, waits for them, and re-layouts  12.6 us (10%)
    pallas_call x1, Pallas kernels, per_device(): pl.pallas_call(functools.partial(step_kernel, dims, params, pairs, blocks...  111 us
    unnamed x7, local copies, waits for them, and re-layouts  10.7 us

profile of v3, /device:TPU:0, one launch (start us, length us, event | category | flops | bytes accessed | tf_op | source)
XLA Modules:
  0.0 124.6 jit_solution(16042250961913007140)
XLA Ops:
  0.6 0.0 copy-start
  0.6 2.4 %copy.10.refs_2_ = bf16[256,1326]{1,0:T(8,128)(2,1)} copy(bf16[256,1326]{0,1:T(8,128)(2,1)} %param.7) | data formatting | bytes 1357824 | tf_op args[1]
  3.0 2.5 %copy.9.refs_1_ = bf16[256,2652]{1,0:T(8,128)(2,1)} copy(bf16[256,2652]{0,1:T(8,128)(2,1)} %param.6) | data formatting | bytes 2715648 | tf_op args[0]
  5.5 0.0 copy-done
  5.5 2.4 %copy.11.refs_5_ = bf16[1536,663]{1,0:T(8,128)(2,1)} copy(bf16[1536,663]{0,1:T(8,128)(2,1)S(1)} %copy-done) | data formatting | bytes 4073472 | tf_op args[5]
  8.0 111.4 %shard_map.85 = (f32[48,2688]{1,0:T(8,128)}, f32[96,768]{1,0:T(8,128)}, f32[96,768]{1,0:T(8,128)}) custom-call(s32[2]{0:T(128)} %refs_0_.1, bf16[256,2652]{1,0:T(8,128)(2,1)} %copy.9.refs_1_, bf16[256,1326]{1,0:T(8,128)(2,1)} %copy.10.refs_2_, bf16[2652,768]{1,0:T(8,128)(2,1)} %refs_3_.1, bf16[768,1536]{1,0:T(8,128)(2,1)} %refs_4_.1, ...), custom_call_target="tpu_custom_call" | custom-call | tf_op jit(solution)/shard_map/pallas_call | solution.py:334
  119.3 1.9 %slice_bitcast_fusion = f32[2652,48]{0,1:T(8,128)} fusion(f32[48,2688]{1,0:T(8,128)} %get-tuple-element.6), kind=kLoop, calls=%fused_computation | loop fusion | bytes 1018368 | tf_op jit(solution)/shard_map/transpose | solution.py:375
  121.2 1.7 %copy.14 = f32[768,96]{0,1:T(8,128)} copy(f32[768,96]{0,1:T(8,128)} %bitcast.5) | data formatting | bytes 589824
  122.9 1.7 %copy.15 = f32[96,663]{1,0:T(8,128)} copy(f32[96,663]{1,0:T(8,128)} %bitcast.4) | data formatting | bytes 509184
Async XLA Ops:
  0.6 4.9 %copy-start = (bf16[1536,663]{0,1:T(8,128)(2,1)S(1)}, bf16[1536,663]{0,1:T(8,128)(2,1)}, u32[]{:S(2)}) copy-start(bf16[1536,663]{0,1:T(8,128)(2,1)} %param.11) | copy-start | bytes 6110212
